TPU v7x, 32 devices: a whole 2x2x4 slice. The times are simulated.
32 devices in a mesh: section: 4 (over z), dp: 8 (over y, x, core).
Axes of the slice: x: 2, y: 2, z: 4, core: 2. Of those that a mesh axis runs over, the one named last changes fastest.
Arguments:
- stream: float32 [2, 64, 16, 16, 128], P(None, 'dp'), may hold values from -6 to 6
- cotangent: float32 [2, 64, 16, 16, 128], P(None, 'dp'), may hold values from -6 to 6
- weights: bfloat16 [4, 2304, 128], P('section'), may hold values from -0.09375 to 0.09375
- master: float32 [4, 2304, 128], P('section', 'dp'), may hold values from -0.09375 to 0.09375
- momentum: float32 [4, 2304, 128], P('section', 'dp'), may hold values from -6 to 6
Outputs:
- new_master: float32 [4, 2304, 128], P('section', 'dp')
- new_momentum: float32 [4, 2304, 128], P('section', 'dp')
- new_weights: bfloat16 [4, 2304, 128], P('section')
All inputs are finite; a program needn't handle non-finite values.
Results may differ from a plain program's by a relative error of at most 0.014.
Values may be sent and summed in bfloat16 or wider, within the bound.
A program may use at most 64 MiB of HBM per device.

v0:
```python
import jax
import jax.numpy as jnp
from jax import lax
from jax.sharding import PartitionSpec as P

LAYERS = 1


step_size = 0.1
inertia = 0.9


def columns(field):
    height = field.shape[1]
    breadth = field.shape[2]
    padded = jnp.pad(jax.nn.silu(field).astype(jnp.bfloat16), ((0, 0), (1, 1), (1, 1), (0, 0)))
    shifted = [
        padded[:, row_tap : row_tap + height, col_tap : col_tap + breadth, :]
        for row_tap in range(3)
        for col_tap in range(3)
    ]
    return jnp.concatenate(shifted, axis=3).reshape(-1, 9 * field.shape[3])


def convolve(patches, weight, template):
    return jnp.dot(patches, weight, preferred_element_type=jnp.float32).reshape(template.shape)


def spread(rounded, weight, template):
    height, breadth, channels = (template.shape[1], template.shape[2], template.shape[3])
    spread_cols = lax.dot_general(
        rounded, weight, (((1,), (1,)), ((), ())), preferred_element_type=jnp.float32
    )
    spread_cols = spread_cols.reshape(template.shape[0], height, breadth, 9 * channels)
    padded = jnp.pad(spread_cols, ((0, 0), (1, 1), (1, 1), (0, 0)))
    summed = jnp.zeros(template.shape, jnp.float32)
    for row_tap in range(3):
        for col_tap in range(3):
            tap_index = 3 * row_tap + col_tap
            summed = (
                summed
                + padded[
                    :,
                    2 - row_tap : 2 - row_tap + height,
                    2 - col_tap : 2 - col_tap + breadth,
                    tap_index * channels : (tap_index + 1) * channels,
                ]
            )
    return summed


def weight_grad(patches, rounded):
    return lax.dot_general(
        patches, rounded, (((0,), (0,)), ((), ())), preferred_element_type=jnp.float32
    )


def silu_slope(field):
    logistic = jax.nn.sigmoid(field)
    return logistic * (1.0 + field * (1.0 - logistic))


def coupling_forward(first, second, weight_f, weight_g):
    patch_f = columns(second)
    out_first = first + convolve(patch_f, weight_f, second)
    patch_g = columns(out_first)
    out_second = second + convolve(patch_g, weight_g, out_first)
    return (out_first, out_second, patch_f, patch_g)


def coupling_grads(
    patch_f, second, patch_g, out_first, grad_first, grad_second, weight_f, weight_g
):
    channels = out_first.shape[3]
    round_second = grad_second.astype(jnp.bfloat16).reshape(-1, channels)
    wgrad_g = weight_grad(patch_g, round_second)
    grad_first = grad_first + spread(round_second, weight_g, out_first) * silu_slope(out_first)
    round_first = grad_first.astype(jnp.bfloat16).reshape(-1, channels)
    wgrad_f = weight_grad(patch_f, round_first)
    grad_second = grad_second + spread(round_first, weight_f, second) * silu_slope(second)
    return (grad_first, grad_second, wgrad_f, wgrad_g)


def coupling_backward(out_first, out_second, grad_first, grad_second, weight_f, weight_g):
    patch_g = columns(out_first)
    second = out_second - convolve(patch_g, weight_g, out_first)
    patch_f = columns(second)
    first = out_first - convolve(patch_f, weight_f, second)
    grad_first, grad_second, wgrad_f, wgrad_g = coupling_grads(
        patch_f, second, patch_g, out_first, grad_first, grad_second, weight_f, weight_g
    )
    return (first, second, grad_first, grad_second, wgrad_f, wgrad_g)


def replicated_grads(stream, cotangent, weights):
    section_index = lax.axis_index("section")
    sections = lax.axis_size("section")
    channels = weights.shape[2]
    gathered = lax.all_gather(weights, "section", axis=0, tiled=True)
    all_blocks = gathered.reshape(sections, LAYERS, 2, 9 * channels, channels)
    share = stream.shape[1] // sections
    own = lax.dynamic_slice_in_dim(stream, section_index * share, share, 1)
    seed = lax.dynamic_slice_in_dim(cotangent, section_index * share, share, 1)

    def forward_one(section_idx, pair):
        blocks = lax.dynamic_index_in_dim(all_blocks, section_idx, 0, keepdims=False)
        first, second = pair
        first, second, patch_f, patch_g = coupling_forward(
            first, second, blocks[0, 0], blocks[0, 1]
        )
        return (first, second)

    first, second = lax.fori_loop(0, sections, forward_one, (own[0], own[1]))

    def backward_one(turn, carry):
        out_first, out_second, grad_first, grad_second, grads = carry
        section_idx = sections - 1 - turn
        blocks = lax.dynamic_index_in_dim(all_blocks, section_idx, 0, keepdims=False)
        pieces = []
        for coupling in reversed(range(LAYERS)):
            out_first, out_second, grad_first, grad_second, wgrad_f, wgrad_g = coupling_backward(
                out_first,
                out_second,
                grad_first,
                grad_second,
                blocks[coupling, 0],
                blocks[coupling, 1],
            )
            pieces.append(jnp.stack([wgrad_f, wgrad_g]))
        pieces = pieces[::-1]
        grads = lax.dynamic_update_index_in_dim(grads, jnp.stack(pieces), section_idx, 0)
        return (out_first, out_second, grad_first, grad_second, grads)

    grads_zero = jnp.zeros((sections, LAYERS, 2, 9 * channels, channels), jnp.float32)
    result = lax.fori_loop(0, sections, backward_one, (first, second, seed[0], seed[1], grads_zero))
    return lax.psum_scatter(
        result[4].reshape(-1, channels), ("section", "dp"), scatter_dimension=0, tiled=True
    )


def on_device(stream, cotangent, weights, master, momentum):
    summed = replicated_grads(stream, cotangent, weights)
    images = stream.shape[1] * lax.axis_size("dp")
    gradient = summed / images
    new_momentum = inertia * momentum[0] + gradient
    new_master = master[0] - step_size * new_momentum
    new_weights = lax.all_gather(new_master.astype(jnp.bfloat16), "dp", axis=0, tiled=True)
    return (new_master[None], new_momentum[None], new_weights[None])


def solution(mesh):
    placed = (
        P(None, "dp", None, None, None),
        P(None, "dp", None, None, None),
        P("section", None, None),
        P("section", "dp", None),
        P("section", "dp", None),
    )
    return jax.shard_map(
        on_device,
        mesh=mesh,
        in_specs=placed,
        out_specs=(P("section", "dp", None), P("section", "dp", None), P("section", None, None)),
        check_vma=False,
    )
```

profile of v0, /device:TPU:0, one launch (start us, length us, event | category | flops | bytes accessed | tf_op | source)
XLA Modules:
  0.0 230.6 jit_solution(14302645406688901209)
XLA Ops:
  7.2 0.7 all-gather.2.cloned.1.call-update
  7.9 1.3 dynamic-slice_bitcast_fusion.2
  9.2 53.1 %all-gather.2.cloned.1.call-done = bf16[4,2304,128]{2,1,0:T(8,128)(2,1)} async-done(((bf16[1,2304,128]{2,1,0:T(8,128)(2,1)}), bf16[4,2304,128]{2,1,0:T(8,128)(2,1)}) %all-gather.2.cloned.1.call-update) | async-done | bytes 2359312 | tf_op jit(solution)/shard_map/all_gather | solution.py:99
  62.3 13.1 %while.40 = (s32[]{:T(128)}, f32[2,16,16,128]{3,2,1,0:T(8,128)S(1)}, f32[2,16,16,128]{3,2,1,0:T(8,128)S(1)}, bf16[4,1,2,1152,128]{4,3,2,1,0:T(8,128)(2,1)}, s32[]{:T(128)}) while((s32[]{:T(128)}, f32[2,16,16,128]{3,2,1,0:T(8,128)S(1)}, f32[2,16,16,128]{3,2,1,0:T(8,128)S(1)}, bf16[4,1,2,1152,128]{4,3,2,1,0:T(8,128)(2,1)}, s32[]{:T(128)}) %tuple.101), condition=%wide.region_1.2_spmd, body=%wide.region_0.1_spmd.sunk | while | flops 303104000 | bytes 10551369 | solution.py:113
  62.4 1.1 dynamic-slice_bitcast_fusion.8
  64.0 0.6 multiply_convert_fusion.7
  65.0 0.5 convolution_add_fusion.3
  65.6 1.1 dynamic-slice_bitcast_fusion.8
  67.3 0.6 multiply_convert_fusion.7
  68.3 0.5 convolution_add_fusion.3
  68.9 1.1 dynamic-slice_bitcast_fusion.8
  70.6 0.6 multiply_convert_fusion.7
  71.6 0.5 convolution_add_fusion.3
  72.2 1.1 dynamic-slice_bitcast_fusion.8
  73.8 0.6 multiply_convert_fusion.7
  74.9 0.5 convolution_add_fusion.3
  75.4 2.5 %broadcast_in_dim.23 = f32[4,1,2,1152,128]{4,3,2,1,0:T(8,128)} broadcast(f32[]{:T(128)} %constant.135.clone.1), dimensions={} | broadcast | bytes 4718596 | tf_op jit(solution)/shard_map/broadcast_in_dim | solution.py:134
  77.9 27.0 %while.41 = (s32[]{:T(128)}, f32[2,16,16,128]{3,2,1,0:T(8,128)S(1)}, f32[2,16,16,128]{3,2,1,0:T(8,128)S(1)}, f32[2,16,16,128]{3,2,1,0:T(8,128)S(1)}, f32[2,16,16...) while((s32[]{:T(128)}, ...), condition=%wide.region_3.4_spmd, body=%wide.region_2.3_spmd.sunk | while | flops 909082624 | bytes 29098156 | solution.py:135
  77.9 1.1 dynamic-slice_bitcast_fusion.9
  80.3 0.5 convolution_bitcast_fusion.4
  80.8 0.5 fusion.149
  81.3 0.7 fusion.158
  82.5 0.5 convolution_subtract_fusion.3
  83.0 0.5 convolution_bitcast_fusion.5
  83.5 1.1 fusion.167
  84.7 1.1 dynamic-slice_bitcast_fusion.9
  87.1 0.5 convolution_bitcast_fusion.4
  87.6 0.5 fusion.149
  88.1 0.7 fusion.158
  89.3 0.5 convolution_subtract_fusion.3
  89.8 0.5 convolution_bitcast_fusion.5
  90.3 1.1 fusion.167
  91.4 1.1 dynamic-slice_bitcast_fusion.9
  93.8 0.5 convolution_bitcast_fusion.4
  94.8 0.7 fusion.158
  96.0 0.5 convolution_subtract_fusion.3
  96.5 0.5 convolution_bitcast_fusion.5
  97.0 1.1 fusion.167
  98.2 1.1 dynamic-slice_bitcast_fusion.9
  100.6 0.5 convolution_bitcast_fusion.4
  101.6 0.7 fusion.158
  102.8 0.5 convolution_subtract_fusion.3
  103.3 0.5 convolution_bitcast_fusion.5
  103.8 1.1 fusion.167
  104.9 106.5 %reduce-scatter.2.cloned.1.call-done = f32[288,128]{1,0:T(8,128)} async-done(((f32[9216,128]{1,0:T(8,128)}), f32[288,128]{1,0:T(8,128)}) %reduce-scatter.2.cloned.1.call-update) | async-done | bytes 147472 | tf_op jit(solution)/shard_map/reduce_scatter | solution.py:136
  211.4 1.7 fusion.61
  213.0 9.9 %all_gather.7 = bf16[2304,128]{1,0:T(8,128)(2,1)S(1)} all-gather(bf16[288,128]{1,0:T(8,128)(2,1)S(1)} %get-tuple-element.339), channel_id=1, replica_groups=mesh['section'=4,'dp'=8] {'dp'}, dimensions={0}, use_global_device_ids=true | all-gather | bytes 663552 | tf_op jit(solution)/shard_map/all_gather | solution.py:147
  223.0 0.8 copy.77
  (169 shorter events, 11.8 us)
Async XLA Ops:
  7.2 55.1 %all-gather.2.cloned.1.call-start = ((), (), s32[]{:S(2)}) async-start(), calls=%async_computation.1 | async-start | bytes 2949120 | tf_op jit(solution)/shard_map/all_gather | solution.py:99
  7.9 203.5 %reduce-scatter.2.cloned.1.call-start = ((), (), s32[]{:S(2)}) async-start(), calls=%async_computation.2 | async-start | bytes 4866048 | tf_op jit(solution)/shard_map/reduce_scatter | solution.py:136
  104.9 106.5 %copy-start = (f32[1,288,128]{2,1,0:T(8,128)S(1)}, f32[1,288,128]{2,1,0:T(8,128)}, u32[]{:S(2)}) copy-start(f32[1,288,128]{2,1,0:T(8,128)} %param.12) | copy-start | bytes 442372
  104.9 106.5 %copy-start.1 = (f32[1,288,128]{2,1,0:T(8,128)S(1)}, f32[1,288,128]{2,1,0:T(8,128)}, u32[]{:S(2)}) copy-start(f32[1,288,128]{2,1,0:T(8,128)} %param.13) | copy-start | bytes 442372
Sparse Core Ops, SparseCore 0:
  9.5 52.6 all-gather.1
  105.0 106.2 reduce-scatter.1
where the time goes:
time: 231 us
  waiting for transfers between devices  160 us (69%)
  local copies, waits for them, and re-layouts  20.2 us (9%)
  matrix products  16.9 us (7%)
  between operations  14.1 us (6%)
  blocking collectives  9.93 us (4%)
  other arithmetic  8.27 us (4%)
    reduce_scatter x1, waiting for transfers between devices, replicated_grads(): lax.psum_scatter(result[4].reshape(-1, channels), ('section', 'dp'), scat...  106 us
    all_gather x1, waiting for transfers between devices, replicated_grads(): gathered = lax.all_gather(weights, 'section', axis=0, tiled=True)  53.1 us
    all_gather x1, blocking collectives, on_device(): lax.all_gather(new_master.astype(jnp.bfloat16), 'dp', axis=0, tiled=True)  9.93 us
    dot_general x16, matrix products, convolve(): jnp.dot(patches, weight, preferred_element_type=jnp.float32)  9.05 us
    while x124, local copies, waits for them, and re-layouts  5.82 us
  transfers between devices with their start and end apart: 2, of which 2 were waited for; matrix products, arithmetic and copies ran while one was open for 1% of the time, Pallas kernels for 0%

commit v1 on v0

v1 whole, which is shorter than its diff:
```python
import functools

import jax
import jax.numpy as jnp
from jax import lax
from jax.experimental import pallas as pl
from jax.experimental.pallas import tpu as pltpu
from jax.sharding import PartitionSpec as P

MESH = pl.DeviceIdType.MESH
step_size = 0.1
inertia = 0.9


def kernel(
    S, D, images,
    stream, cotangent, weights, master, momentum,
    new_master, new_momentum, new_weights,
    wbuf, xs, ds, pads, kept, slopes, g32, gsend, recv1, zsend, recv2, gown, wsend,
    in_sem, own_sem, wsend_sem, wrecv_sem, fsend_sem, frecv_sem,
    gsend_sem, grecv_sem, zsend_sem, zrecv_sem, osend_sem, orecv_sem,
):
    s = lax.axis_index("section")
    d = lax.axis_index("dp")
    half = lax.rem(d, 2)
    partner = d + 1 - 2 * half
    share, H, W, C = xs.shape[1:]
    M = share * H * W
    rows = master.shape[0]

    def weight_copy(sec_from, to):
        return pltpu.make_async_remote_copy(
            src_ref=weights.at[half], dst_ref=wbuf.at[sec_from, half],
            send_sem=wsend_sem.at[to], recv_sem=wrecv_sem.at[sec_from],
            device_id=(to, d), device_id_type=MESH)

    def forward_copy(sec, which):
        return pltpu.make_async_remote_copy(
            src_ref=wbuf.at[sec, which], dst_ref=wbuf.at[sec, which],
            send_sem=fsend_sem.at[sec], recv_sem=frecv_sem.at[sec],
            device_id=(s, partner), device_id_type=MESH)

    for i in range(1, S):
        weight_copy(s, lax.rem(s + i, S)).start()
    load_own = pltpu.make_async_copy(weights, wbuf.at[s], own_sem)
    load_own.start()
    mine = pl.ds(s * share, share)
    loads = [
        pltpu.make_async_copy(stream.at[0, mine], xs.at[0], in_sem.at[0]),
        pltpu.make_async_copy(stream.at[1, mine], xs.at[1], in_sem.at[1]),
        pltpu.make_async_copy(cotangent.at[0, mine], ds.at[0], in_sem.at[2]),
        pltpu.make_async_copy(cotangent.at[1, mine], ds.at[1], in_sem.at[3]),
    ]
    for load in loads:
        load.start()

    zero_row = jnp.zeros((share, 1, W, 3 * C), jnp.bfloat16)
    for k in range(2):
        pads[k, :, 0:1] = zero_row
        pads[k, :, H + 1 : H + 2] = zero_row

    col = lax.rem(lax.broadcasted_iota(jnp.int32, (M, C), 0), W)

    def shifted(k, flat, order):
        before = jnp.where(col == 0, 0.0, pltpu.roll(flat, 1, 0))
        after = jnp.where(col == W - 1, 0.0, pltpu.roll(flat, M - 1, 0))
        for b, piece in enumerate((before, flat, after) if order else (after, flat, before)):
            pads[k, :, 1 : H + 1, :, b * C : (b + 1) * C] = piece.astype(jnp.bfloat16).reshape(
                share, H, W, C)

    def activate(value, sec, which):
        logistic = 1.0 / (1.0 + jnp.exp(-value))
        act = value * logistic
        slopes[sec, which] = logistic * (1.0 + value * (1.0 - logistic))
        kept[sec, which] = act.astype(jnp.bfloat16)
        shifted(0, act, True)

    def conv(sec, which):
        total = jnp.zeros((M, C), jnp.float32)
        for a in range(3):
            total += jnp.dot(
                pads[0, :, a : a + H].reshape(M, 3 * C),
                wbuf[sec, which, a * 3 * C : (a + 1) * 3 * C],
                preferred_element_type=jnp.float32)
        return total

    def pass_on(sec):
        @pl.when(sec != s)
        def _():
            weight_copy(sec, s).wait_recv()
            forward_copy(sec, half).start()

    def take(sec):
        @pl.when(sec != s)
        def _():
            forward_copy(sec, 1 - half).wait_recv()

    load_own.wait()
    for load in loads:
        load.wait()
    pass_on(0)

    def forward_one(sec, carry):
        first = xs[0].reshape(M, C)
        second = xs[1].reshape(M, C)
        activate(second, sec, 0)
        take(sec)
        first = first + conv(sec, 0)
        activate(first, sec, 1)
        xs[0] = first.reshape(share, H, W, C)

        @pl.when(sec + 1 < S)
        def _():
            pass_on(sec + 1)

        xs[1] = (second + conv(sec, 1)).reshape(share, H, W, C)
        return carry

    lax.fori_loop(0, S, forward_one, 0)

    def grad_copy(sec, src, to):
        return pltpu.make_async_remote_copy(
            src_ref=gsend.at[sec, to], dst_ref=recv1.at[sec, src],
            send_sem=gsend_sem.at[sec, to], recv_sem=grecv_sem.at[sec, src],
            device_id=(s, to), device_id_type=MESH)

    def sum_copy(sec, src):
        return pltpu.make_async_remote_copy(
            src_ref=zsend.at[sec], dst_ref=recv2.at[src],
            send_sem=zsend_sem.at[sec], recv_sem=zrecv_sem.at[src],
            device_id=(sec, d), device_id_type=MESH)

    def grads(sec, which):
        rounded = ds[1 if which else 0].reshape(M, C)
        shifted(1, rounded, False)
        act = kept[sec, which]
        for a in range(3):
            block = lax.dot_general(
                act, pads[1, :, 2 - a : 2 - a + H].reshape(M, 3 * C),
                (((0,), (0,)), ((), ())), preferred_element_type=jnp.float32)
            for b in range(3):
                g32[(3 * a + b) * C : (3 * a + b + 1) * C] = block[:, b * C : (b + 1) * C]
        per = D // 2

        def send(i, carry):
            at = lax.rem(i + d, per)
            to = which * per + at
            gsend[sec, to] = g32[pl.ds(pl.multiple_of(at * rows, 8), rows)].astype(jnp.bfloat16)

            @pl.when(to != d)
            def _():
                grad_copy(sec, d, to).start()
            return carry

        lax.fori_loop(0, per, send, 0)
        total = jnp.zeros((M, C), jnp.float32)
        for a in range(3):
            for b in range(3):
                tap = 3 * a + b
                total += lax.dot_general(
                    pads[1, :, 2 - a : 2 - a + H, :, b * C : (b + 1) * C].reshape(M, C),
                    wbuf[sec, which, tap * C : (tap + 1) * C],
                    (((1,), (1,)), ((), ())), preferred_element_type=jnp.float32)
        into = 0 if which else 1
        ds[into] = ds[into] + (total * slopes[sec, which]).reshape(share, H, W, C)

    def finish(sec):
        def add(i, total):
            src = lax.rem(d + i, D)
            grad_copy(sec, src, d).wait_recv()
            return total + recv1[sec, src].astype(jnp.float32)

        total = lax.fori_loop(1, D, add, gsend[sec, d].astype(jnp.float32))

        @pl.when(sec == s)
        def _():
            gown[...] = total

        @pl.when(sec != s)
        def _():
            zsend[sec] = total.astype(jnp.bfloat16)
            sum_copy(sec, s).start()

    def backward_one(turn, carry):
        sec = S - 1 - turn
        grads(sec, 1)

        @pl.when(turn > 0)
        def _():
            finish(sec + 1)

        grads(sec, 0)
        return carry

    lax.fori_loop(0, S, backward_one, 0)
    finish(0)

    def gather_sums(i, total):
        src = lax.rem(s + i, S)
        sum_copy(s, src).wait_recv()
        return total + recv2[src].astype(jnp.float32)

    summed = lax.fori_loop(1, S, gather_sums, gown[...])
    moved = inertia * momentum[...] + summed / images
    new_momentum[...] = moved
    fresh = master[...] - step_size * moved
    new_master[...] = fresh
    wsend[...] = fresh.astype(jnp.bfloat16)

    def out_copy(src, to):
        return pltpu.make_async_remote_copy(
            src_ref=wsend, dst_ref=new_weights.at[src],
            send_sem=osend_sem.at[to], recv_sem=orecv_sem.at[src],
            device_id=(s, to), device_id_type=MESH)

    @pl.loop(1, D)
    def _(i):
        out_copy(d, lax.rem(d + i, D)).start()

    keep_own = pltpu.make_async_copy(wsend, new_weights.at[d], own_sem)
    keep_own.start()

    @pl.loop(1, S)
    def _(i):
        other = lax.rem(s + i, S)
        weight_copy(s, other).wait_send()
        forward_copy(other, half).wait_send()
        sum_copy(other, s).wait_send()

    @pl.loop(0, S)
    def _(sec):
        @pl.loop(1, D)
        def _(i):
            grad_copy(sec, d, lax.rem(d + i, D)).wait_send()

    keep_own.wait()

    @pl.loop(1, D)
    def _(i):
        other = lax.rem(d + i, D)
        out_copy(d, other).wait_send()
        out_copy(other, d).wait_recv()


def on_device(S, D, stream, cotangent, weights, master, momentum):
    _, per_dp, H, W, C = stream.shape
    share = per_dp // S
    M = share * H * W
    R = weights.shape[1]
    rows = master.shape[1]
    bf, f32 = jnp.bfloat16, jnp.float32
    vmem = pl.BlockSpec(memory_space=pltpu.VMEM)
    hbm = pl.BlockSpec(memory_space=pl.ANY)
    dma = pltpu.SemaphoreType.DMA
    new_master, new_momentum, new_weights = pl.pallas_call(
        functools.partial(kernel, S, D, per_dp * D),
        out_shape=(
            jax.ShapeDtypeStruct((rows, C), f32),
            jax.ShapeDtypeStruct((rows, C), f32),
            jax.ShapeDtypeStruct((D, rows, C), bf),
        ),
        in_specs=[hbm, hbm, hbm, vmem, vmem],
        out_specs=(vmem, vmem, hbm),
        scratch_shapes=[
            pltpu.VMEM((S, 2, R // 2, C), bf),
            pltpu.VMEM((2, share, H, W, C), f32),
            pltpu.VMEM((2, share, H, W, C), f32),
            pltpu.VMEM((2, share, H + 2, W, 3 * C), bf),
            pltpu.VMEM((S, 2, M, C), bf),
            pltpu.VMEM((S, 2, M, C), f32),
            pltpu.VMEM((R // 2, C), f32),
            pltpu.VMEM((S, D, rows, C), bf),
            pltpu.VMEM((S, D, rows, C), bf),
            pltpu.VMEM((S, rows, C), bf),
            pltpu.VMEM((S, rows, C), bf),
            pltpu.VMEM((rows, C), f32),
            pltpu.VMEM((rows, C), bf),
            dma((4,)), dma, dma((S,)), dma((S,)), dma((S,)), dma((S,)),
            dma((S, D)), dma((S, D)), dma((S,)), dma((S,)), dma((D,)), dma((D,)),
        ],
        compiler_params=pltpu.CompilerParams(
            has_side_effects=True, vmem_limit_bytes=48 * 1024 * 1024),
    )(stream, cotangent, weights.reshape(2, R // 2, C), master[0], momentum[0])
    return (new_master[None], new_momentum[None], new_weights.reshape(1, R, C))


def solution(mesh):
    placed = (
        P(None, "dp", None, None, None),
        P(None, "dp", None, None, None),
        P("section", None, None),
        P("section", "dp", None),
        P("section", "dp", None),
    )
    return jax.shard_map(
        functools.partial(on_device, mesh.shape["section"], mesh.shape["dp"]),
        mesh=mesh,
        in_specs=placed,
        out_specs=(P("section", "dp", None), P("section", "dp", None), P("section", None, None)),
        check_vma=False,
    )
```

time: 231 us -> 94.5 us (0.41)
  waiting for transfers between devices: 160 us -> 0 us
  Pallas kernels: 0 us -> 85.2 us
  matrix products: 16.9 us -> 0 us
  between operations: 14.1 us -> 0.65 us
  local copies, waits for them, and re-layouts: 20.2 us -> 8.2 us
  blocking collectives: 9.93 us -> 0 us
  other arithmetic: 8.27 us -> 0 us
    reduce_scatter x1 -> x0, waiting for transfers between devices: 106 us -> none  [replicated_grads(): lax.psum_scatter(result[4].reshape(-1, channels), ('section', 'dp'), scat...]
    pallas_call x0 -> x1, Pallas kernels: none -> 85.2 us  [on_device(): pl.pallas_call(functools.partial(kernel, S, D, per_dp * D), out_shape=(ja...]
    all_gather x1 -> x0, waiting for transfers between devices: 53.1 us -> none  [replicated_grads(): gathered = lax.all_gather(weights, 'section', axis=0, tiled=True)]
    dot_general x32 -> x0, matrix products: 16.9 us -> none  [the longest x16 9.05 us: convolve(): jnp.dot(patches, weight, preferred_element_type=jnp.float32)]
    squeeze x9 -> x0, local copies, waits for them, and re-layouts: 10.1 us -> none  [the longest x4 4.44 us: forward_one(): lax.dynamic_index_in_dim(all_blocks, section_idx, 0, keepdims=False)]
    all_gather x1 -> x0, blocking collectives: 9.93 us -> none  [on_device(): lax.all_gather(new_master.astype(jnp.bfloat16), 'dp', axis=0, tiled=True)]
    unnamed x5 -> x13, local copies, waits for them, and re-layouts: 0.82 us -> 8.2 us
    while x124 -> x0, local copies, waits for them, and re-layouts: 5.82 us -> none
  transfers between devices with their start and end apart: 2 -> 0, of which waited for: 2 -> 0; matrix products, arithmetic and copies ran while one was open for 1% -> 0% of each run, Pallas kernels for 0% -> 0%
where the time goes in v1:
time: 94.5 us; the launch traced here: 94.1 us
  Pallas kernels  85.2 us (90%)
  local copies, waits for them, and re-layouts  8.2 us (9%)
    pallas_call x1, Pallas kernels, on_device(): pl.pallas_call(functools.partial(kernel, S, D, per_dp * D), out_shape=(ja...  85.2 us
    unnamed x13, local copies, waits for them, and re-layouts  8.2 us

profile of v1, /device:TPU:0, one launch (start us, length us, event | category | flops | bytes accessed | tf_op | source)
XLA Modules:
  0.0 94.1 jit_solution(14581096813192915715)
XLA Ops:
  0.6 0.0 copy-start
  0.6 1.6 %copy-done = f32[2,8,16,16,128]{4,3,2,1,0:T(8,128)S(1)} copy-done((f32[2,8,16,16,128]{4,3,2,1,0:T(8,128)S(1)}, f32[2,8,16,16,128]{4,3,2,1,0:T(8,128)}, u32[]{:S(2)}) %copy-start) | copy-done | bytes 2097176
  2.2 0.0 copy-start.1
  2.2 1.6 %copy-done.1 = f32[2,8,16,16,128]{4,3,2,1,0:T(8,128)S(1)} copy-done((f32[2,8,16,16,128]{4,3,2,1,0:T(8,128)S(1)}, f32[2,8,16,16,128]{4,3,2,1,0:T(8,128)}, u32[]{:S(2)}) %copy-start.1) | copy-done | bytes 2097176
  3.8 0.0 copy-start.2
  3.8 1.1 %copy-done.2 = bf16[1,2304,128]{2,1,0:T(8,128)(2,1)S(1)} copy-done((bf16[1,2304,128]{2,1,0:T(8,128)(2,1)S(1)}, bf16[1,2304,128]{2,1,0:T(8,128)(2,1)}, u32[]{:S(2)}) %copy-start.2) | copy-done | bytes 589848
  4.9 0.0 copy-start.3
  4.9 0.9 copy-done.3
  5.8 0.0 copy-start.4
  5.8 0.9 copy-done.4
  6.7 85.2 %shard_map.76 = (f32[288,128]{1,0:T(8,128)S(1)}, f32[288,128]{1,0:T(8,128)S(1)}, bf16[8,288,128]{2,1,0:T(8,128)(2,1)S(1)}) custom-call(f32[2,8,16,16,128]{4,3,2,1,0:T(8,128)S(1)} %copy-done, f32[2,8,16,16,128]{4,3,2,1,0:T(8,128)S(1)} %copy-done.1, bf16[2,1152,128]{2,1,0:T(8,128)(2,1)S(1)} %bitcast.6, f32[288,128]{1,0:T(8,128)S(1)} %bitcast.8, ...), custom_call_target="tpu_custom_call" | custom-call | tf_op jit(solution)/shard_map/pallas_call | solution.py:255
  92.0 0.7 copy.11
  92.6 0.7 copy.12
  93.3 0.8 copy.13
Async XLA Ops:
  0.6 1.6 %copy-start = (f32[2,8,16,16,128]{4,3,2,1,0:T(8,128)S(1)}, f32[2,8,16,16,128]{4,3,2,1,0:T(8,128)}, u32[]{:S(2)}) copy-start(f32[2,8,16,16,128]{4,3,2,1,0:T(8,128)} %stream.1) | copy-start | bytes 6291460
  2.2 1.6 %copy-start.1 = (f32[2,8,16,16,128]{4,3,2,1,0:T(8,128)S(1)}, f32[2,8,16,16,128]{4,3,2,1,0:T(8,128)}, u32[]{:S(2)}) copy-start(f32[2,8,16,16,128]{4,3,2,1,0:T(8,128)} %cotangent.1) | copy-start | bytes 6291460
  3.8 1.1 %copy-start.2 = (bf16[1,2304,128]{2,1,0:T(8,128)(2,1)S(1)}, bf16[1,2304,128]{2,1,0:T(8,128)(2,1)}, u32[]{:S(2)}) copy-start(bf16[1,2304,128]{2,1,0:T(8,128)(2,1)} %param.7) | copy-start | bytes 1769476
  4.9 0.9 copy-start.3
  5.8 0.9 copy-start.4

commit v2 on v1

--- a/solution.py
+++ b/solution.py
@@ -1,4 +1,5 @@
 import functools
+import math
 
 import jax
 import jax.numpy as jnp
@@ -16,32 +17,52 @@
     S, D, images,
     stream, cotangent, weights, master, momentum,
     new_master, new_momentum, new_weights,
-    wbuf, xs, ds, pads, kept, slopes, g32, gsend, recv1, zsend, recv2, gown, wsend,
-    in_sem, own_sem, wsend_sem, wrecv_sem, fsend_sem, frecv_sem,
-    gsend_sem, grecv_sem, zsend_sem, zrecv_sem, osend_sem, orecv_sem,
+    wbuf, xs, ds, pads, kept, slopes, g32, gsend, pairs, recv1, zsend, recv2, gown, spread_out,
+    in_sem, own_sem, w1send, w1recv, w2send, w2recv, w3send, w3recv,
+    psend, precv, gsend_sem, grecv_sem, zsend_sem, zrecv_sem,
+    osend_sem, orecv_sem, fsend_sem, frecv_sem,
 ):
     s = lax.axis_index("section")
     d = lax.axis_index("dp")
-    half = lax.rem(d, 2)
-    partner = d + 1 - 2 * half
+    core = lax.rem(d, 2)
+    partner = d + 1 - 2 * core
+    chips = D // 2
     share, H, W, C = xs.shape[1:]
     M = share * H * W
     rows = master.shape[0]
-
-    def weight_copy(sec_from, to):
-        return pltpu.make_async_remote_copy(
-            src_ref=weights.at[half], dst_ref=wbuf.at[sec_from, half],
-            send_sem=wsend_sem.at[to], recv_sem=wrecv_sem.at[sec_from],
+    R = rows * D
+    NC = math.gcd(R // 16, D)
+    part = R // NC
+
+    def chunk(i):
+        return pl.ds(pl.multiple_of(i * part, 16), part)
+
+    def other_chip(i):
+        return lax.rem(d + 2 * i, D)
+
+    def section_copy(src, to):
+        return pltpu.make_async_remote_copy(
+            src_ref=weights.at[chunk(d)], dst_ref=wbuf.at[src, chunk(d)],
+            send_sem=w1send.at[to], recv_sem=w1recv.at[src],
             device_id=(to, d), device_id_type=MESH)
 
-    def forward_copy(sec, which):
-        return pltpu.make_async_remote_copy(
-            src_ref=wbuf.at[sec, which], dst_ref=wbuf.at[sec, which],
-            send_sem=fsend_sem.at[sec], recv_sem=frecv_sem.at[sec],
+    def layer_copy(sec, src, to):
+        return pltpu.make_async_remote_copy(
+            src_ref=wbuf.at[sec, chunk(src)], dst_ref=wbuf.at[sec, chunk(src)],
+            send_sem=w2send.at[sec, to], recv_sem=w2recv.at[sec, src],
+            device_id=(s, to), device_id_type=MESH)
+
+    def core_copy(sec, src):
+        return pltpu.make_async_remote_copy(
+            src_ref=wbuf.at[sec, chunk(src)], dst_ref=wbuf.at[sec, chunk(src)],
+            send_sem=w3send.at[sec, src], recv_sem=w3recv.at[sec, src],
             device_id=(s, partner), device_id_type=MESH)
 
-    for i in range(1, S):
-        weight_copy(s, lax.rem(s + i, S)).start()
+    @pl.when(d < NC)
+    def _():
+        for i in range(1, S):
+            section_copy(s, lax.rem(s + i, S)).start()
+
     load_own = pltpu.make_async_copy(weights, wbuf.at[s], own_sem)
     load_own.start()
     mine = pl.ds(s * share, share)
@@ -80,24 +101,52 @@
         for a in range(3):
             total += jnp.dot(
                 pads[0, :, a : a + H].reshape(M, 3 * C),
-                wbuf[sec, which, a * 3 * C : (a + 1) * 3 * C],
+                wbuf[sec, which * 9 * C + a * 3 * C : which * 9 * C + (a + 1) * 3 * C],
                 preferred_element_type=jnp.float32)
         return total
 
+    def relay(sec):
+        @pl.when((sec != s) & (d < NC))
+        def _():
+            section_copy(sec, s).wait_recv()
+            layer_copy(sec, d, partner).start()
+
+            @pl.loop(1, chips)
+            def _(i):
+                layer_copy(sec, d, other_chip(i)).start()
+
     def pass_on(sec):
         @pl.when(sec != s)
         def _():
-            weight_copy(sec, s).wait_recv()
-            forward_copy(sec, half).start()
+            @pl.loop(1, chips)
+            def _(i):
+                src = other_chip(i)
+
+                @pl.when(src < NC)
+                def _():
+                    layer_copy(sec, src, d).wait_recv()
+                    core_copy(sec, src).start()
 
     def take(sec):
         @pl.when(sec != s)
         def _():
-            forward_copy(sec, 1 - half).wait_recv()
+            @pl.when(partner < NC)
+            def _():
+                layer_copy(sec, partner, d).wait_recv()
+
+            @pl.loop(1, chips)
+            def _(i):
+                src = lax.rem(partner + 2 * i, D)
+
+                @pl.when(src < NC)
+                def _():
+                    core_copy(sec, src).wait_recv()
 
     load_own.wait()
     for load in loads:
         load.wait()
+    for sec in range(S):
+        relay(sec)
     pass_on(0)
 
     def forward_one(sec, carry):
@@ -117,6 +166,12 @@
         return carry
 
     lax.fori_loop(0, S, forward_one, 0)
+
+    def pair_copy(sec, to):
+        return pltpu.make_async_remote_copy(
+            src_ref=gsend.at[sec, to], dst_ref=pairs.at[sec, to],
+            send_sem=psend.at[sec, to], recv_sem=precv.at[sec, to],
+            device_id=(s, partner), device_id_type=MESH)
 
     def grad_copy(sec, src, to):
         return pltpu.make_async_remote_copy(
@@ -142,35 +197,52 @@
                 g32[(3 * a + b) * C : (3 * a + b + 1) * C] = block[:, b * C : (b + 1) * C]
         per = D // 2
 
-        def send(i, carry):
-            at = lax.rem(i + d, per)
-            to = which * per + at
-            gsend[sec, to] = g32[pl.ds(pl.multiple_of(at * rows, 8), rows)].astype(jnp.bfloat16)
-
-            @pl.when(to != d)
-            def _():
-                grad_copy(sec, d, to).start()
-            return carry
-
-        lax.fori_loop(0, per, send, 0)
+        def convert(at):
+            gsend[sec, which * per + at] = g32[
+                pl.ds(pl.multiple_of(at * rows, 8), rows)].astype(jnp.bfloat16)
+
+        @pl.loop(0, per // 2)
+        def _(i):
+            at = 2 * i + 1 - core
+            convert(at)
+            pair_copy(sec, which * per + at).start()
+
+        @pl.loop(0, per // 2)
+        def _(i):
+            convert(2 * i + core)
+
         total = jnp.zeros((M, C), jnp.float32)
         for a in range(3):
             for b in range(3):
                 tap = 3 * a + b
                 total += lax.dot_general(
                     pads[1, :, 2 - a : 2 - a + H, :, b * C : (b + 1) * C].reshape(M, C),
-                    wbuf[sec, which, tap * C : (tap + 1) * C],
+                    wbuf[sec, which * 9 * C + tap * C : which * 9 * C + (tap + 1) * C],
                     (((1,), (1,)), ((), ())), preferred_element_type=jnp.float32)
         into = 0 if which else 1
         ds[into] = ds[into] + (total * slopes[sec, which]).reshape(share, H, W, C)
 
+    def combine(sec, which):
+        per = D // 2
+
+        @pl.loop(0, per // 2)
+        def _(i):
+            to = which * per + 2 * i + core
+            pair_copy(sec, to).wait_recv()
+            both = gsend[sec, to].astype(jnp.float32) + pairs[sec, to].astype(jnp.float32)
+            gsend[sec, to] = both.astype(jnp.bfloat16)
+
+            @pl.when(to != d)
+            def _():
+                grad_copy(sec, d, to).start()
+
     def finish(sec):
         def add(i, total):
-            src = lax.rem(d + i, D)
+            src = other_chip(i)
             grad_copy(sec, src, d).wait_recv()
             return total + recv1[sec, src].astype(jnp.float32)
 
-        total = lax.fori_loop(1, D, add, gsend[sec, d].astype(jnp.float32))
+        total = lax.fori_loop(1, chips, add, gsend[sec, d].astype(jnp.float32))
 
         @pl.when(sec == s)
         def _():
@@ -184,12 +256,14 @@
     def backward_one(turn, carry):
         sec = S - 1 - turn
         grads(sec, 1)
+        combine(sec, 1)
 
         @pl.when(turn > 0)
         def _():
             finish(sec + 1)
 
         grads(sec, 0)
+        combine(sec, 0)
         return carry
 
     lax.fori_loop(0, S, backward_one, 0)
@@ -205,41 +279,72 @@
     new_momentum[...] = moved
     fresh = master[...] - step_size * moved
     new_master[...] = fresh
-    wsend[...] = fresh.astype(jnp.bfloat16)
+    spread_out[d] = fresh.astype(jnp.bfloat16)
 
     def out_copy(src, to):
         return pltpu.make_async_remote_copy(
-            src_ref=wsend, dst_ref=new_weights.at[src],
+            src_ref=spread_out.at[src], dst_ref=spread_out.at[src],
             send_sem=osend_sem.at[to], recv_sem=orecv_sem.at[src],
             device_id=(s, to), device_id_type=MESH)
 
-    @pl.loop(1, D)
+    def hand_over(src):
+        return pltpu.make_async_remote_copy(
+            src_ref=spread_out.at[src], dst_ref=spread_out.at[src],
+            send_sem=fsend_sem.at[src], recv_sem=frecv_sem.at[src],
+            device_id=(s, partner), device_id_type=MESH)
+
+    @pl.loop(1, chips)
     def _(i):
-        out_copy(d, lax.rem(d + i, D)).start()
-
-    keep_own = pltpu.make_async_copy(wsend, new_weights.at[d], own_sem)
-    keep_own.start()
+        out_copy(d, other_chip(i)).start()
+
+    out_copy(d, partner).start()
 
     @pl.loop(1, S)
     def _(i):
         other = lax.rem(s + i, S)
-        weight_copy(s, other).wait_send()
-        forward_copy(other, half).wait_send()
         sum_copy(other, s).wait_send()
+
+        @pl.when(d < NC)
+        def _():
+            section_copy(s, other).wait_send()
+            layer_copy(other, d, partner).wait_send()
+
+        @pl.loop(1, chips)
+        def _(j):
+            @pl.when(d < NC)
+            def _():
+                layer_copy(other, d, other_chip(j)).wait_send()
+
+            @pl.when(other_chip(j) < NC)
+            def _():
+                core_copy(other, other_chip(j)).wait_send()
 
     @pl.loop(0, S)
     def _(sec):
-        @pl.loop(1, D)
+        @pl.loop(1, chips)
         def _(i):
-            grad_copy(sec, d, lax.rem(d + i, D)).wait_send()
-
-    keep_own.wait()
-
-    @pl.loop(1, D)
+            grad_copy(sec, d, other_chip(i)).wait_send()
+
+        @pl.loop(0, chips)
+        def _(i):
+            pair_copy(sec, 2 * i + 1 - core).wait_send()
+
+    @pl.loop(1, chips)
     def _(i):
-        other = lax.rem(d + i, D)
-        out_copy(d, other).wait_send()
-        out_copy(other, d).wait_recv()
+        src = other_chip(i)
+        out_copy(src, d).wait_recv()
+        hand_over(src).start()
+
+    out_copy(partner, d).wait_recv()
+    out_copy(d, partner).wait_send()
+
+    @pl.loop(1, chips)
+    def _(i):
+        out_copy(d, other_chip(i)).wait_send()
+        hand_over(other_chip(i)).wait_send()
+        hand_over(lax.rem(partner + 2 * i, D)).wait_recv()
+
+    new_weights[...] = spread_out[...]
 
 
 def on_device(S, D, stream, cotangent, weights, master, momentum):
@@ -260,9 +365,9 @@
             jax.ShapeDtypeStruct((D, rows, C), bf),
         ),
         in_specs=[hbm, hbm, hbm, vmem, vmem],
-        out_specs=(vmem, vmem, hbm),
+        out_specs=(vmem, vmem, vmem),
         scratch_shapes=[
-            pltpu.VMEM((S, 2, R // 2, C), bf),
+            pltpu.VMEM((S, R, C), bf),
             pltpu.VMEM((2, share, H, W, C), f32),
             pltpu.VMEM((2, share, H, W, C), f32),
             pltpu.VMEM((2, share, H + 2, W, 3 * C), bf),
@@ -271,16 +376,18 @@
             pltpu.VMEM((R // 2, C), f32),
             pltpu.VMEM((S, D, rows, C), bf),
             pltpu.VMEM((S, D, rows, C), bf),
+            pltpu.VMEM((S, D, rows, C), bf),
             pltpu.VMEM((S, rows, C), bf),
             pltpu.VMEM((S, rows, C), bf),
             pltpu.VMEM((rows, C), f32),
-            pltpu.VMEM((rows, C), bf),
-            dma((4,)), dma, dma((S,)), dma((S,)), dma((S,)), dma((S,)),
-            dma((S, D)), dma((S, D)), dma((S,)), dma((S,)), dma((D,)), dma((D,)),
+            pltpu.VMEM((D, rows, C), bf),
+            dma((4,)), dma, dma((S,)), dma((S,)), dma((S, D)), dma((S, D)), dma((S, D)), dma((S, D)),
+            dma((S, D)), dma((S, D)), dma((S, D)), dma((S, D)), dma((S,)), dma((S,)),
+            dma((D,)), dma((D,)), dma((D,)), dma((D,)),
         ],
         compiler_params=pltpu.CompilerParams(
-            has_side_effects=True, vmem_limit_bytes=48 * 1024 * 1024),
-    )(stream, cotangent, weights.reshape(2, R // 2, C), master[0], momentum[0])
+            has_side_effects=True, vmem_limit_bytes=61 * 1024 * 1024),
+    )(stream, cotangent, weights[0], master[0], momentum[0])
     return (new_master[None], new_momentum[None], new_weights.reshape(1, R, C))
 
 

time: 94.5 us -> 76.4 us (0.81)
  Pallas kernels: 85.2 us -> 70.5 us
  local copies, waits for them, and re-layouts: 8.2 us -> 5.08 us
    pallas_call x1, Pallas kernels: 85.2 us -> 70.5 us  [on_device(): pl.pallas_call(functools.partial(kernel, S, D, per_dp * D), out_shape=(ja...]
    unnamed x13 -> x3, local copies, waits for them, and re-layouts: 8.2 us -> 5.08 us
where the time goes in v2:
time: 76.4 us; the launch traced here: 76.2 us
  Pallas kernels  70.5 us (92%)
  local copies, waits for them, and re-layouts  5.08 us (7%)
    pallas_call x1, Pallas kernels, on_device(): pl.pallas_call(functools.partial(kernel, S, D, per_dp * D), out_shape=(ja...  70.5 us
    unnamed x3, local copies, waits for them, and re-layouts  5.08 us

profile of v2, /device:TPU:0, one launch (start us, length us, event | category | flops | bytes accessed | tf_op | source)
XLA Modules:
  0.0 76.2 jit_solution(3167606085612372467)
XLA Ops:
  0.6 70.5 %shard_map.76 = (f32[288,128]{1,0:T(8,128)}, f32[288,128]{1,0:T(8,128)}, bf16[8,288,128]{2,1,0:T(8,128)(2,1)}) custom-call(f32[2,8,16,16,128]{4,3,2,1,0:T(8,128)} %stream.1, f32[2,8,16,16,128]{4,3,2,1,0:T(8,128)} %cotangent.1, bf16[2304,128]{1,0:T(8,128)(2,1)} %bitcast.6, f32[288,128]{1,0:T(8,128)} %bitcast.8, f32[288,128]{1,0:T(8,128)} %bitcast.9), custom_call_target="tpu_custom_call" | custom-call | tf_op jit(solution)/shard_map/pallas_call | solution.py:360
  71.1 1.6 %copy.11 = f32[1,288,128]{2,1,0:T(8,128)} copy(f32[1,288,128]{2,1,0:T(8,128)} %bitcast.11) | data formatting | bytes 294912
  72.7 1.6 %copy.12 = f32[1,288,128]{2,1,0:T(8,128)} copy(f32[1,288,128]{2,1,0:T(8,128)} %bitcast.10) | data formatting | bytes 294912
  74.3 1.9 %copy.13 = bf16[1,2304,128]{2,1,0:T(8,128)(2,1)} copy(bf16[1,2304,128]{2,1,0:T(8,128)(2,1)} %bitcast.7) | data formatting | bytes 1179648
